TPU v7x, 256 devices: a whole 4x4x8 slice. The times are simulated.
256 devices in a mesh: ga: 16 (over x_hi, y, core), band: 16 (over x_lo, z).
Axes of the slice: x: 4 (x_hi: 2, x_lo: 2; x = x_hi * 2 + x_lo), y: 4, z: 8, core: 2. Of those that a mesh axis runs over, the one named last changes fastest.
Arguments:
- waves: bfloat16 [2, 16384, 4096], P(None, 'ga', 'band'), may hold values from -6 to 6
- rotation: bfloat16 [2, 4096, 4096], P(None, 'ga', 'band'), may hold values from -0.0625 to 0.0625
Outputs:
- rotated: bfloat16 [2, 16384, 4096], P(None, 'ga', 'band')
All inputs are finite; a program needn't handle non-finite values.
Results may differ from a plain program's by a relative error of at most 0.001.
Values may be sent and summed in bfloat16 or wider, within the bound.
A program may use at most 128 MiB of HBM per device.

v0:
```python
import jax
import jax.numpy as jnp
from jax import lax
from jax.sharding import Mesh
from jax.sharding import PartitionSpec as P

GA = ("ga_0", "ga_1", "ga_2")


def sent_to_all(array, axis):
    copies = jnp.broadcast_to(array, (lax.axis_size(axis), *array.shape))
    return lax.all_to_all(copies, axis, split_axis=0, concat_axis=0, tiled=True)


def laid_out(blocks, dim):
    blocks = jnp.moveaxis(blocks, 0, dim)
    lengths = blocks.shape
    return blocks.reshape(*lengths[:dim], lengths[dim] * lengths[dim + 1], *lengths[dim + 2 :])


def whole_of(array, axes, dim):
    far, near = axes
    blocks = sent_to_all(sent_to_all(array, far), near)
    return laid_out(blocks.swapaxes(0, 1).reshape(-1, *array.shape), dim)


def local(waves, rotation):
    cols_here = waves.shape[2]
    columns = whole_of(rotation, (("ga_0", "ga_1"), "ga_2"), 1)
    real_rows = jnp.concatenate([columns[0], columns[1]], axis=1)
    imag_rows = jnp.concatenate([-columns[1], columns[0]], axis=1)
    piece = lax.all_gather(waves, "band", axis=2, tiled=True)
    total = jnp.dot(piece[0], real_rows, preferred_element_type=jnp.float32)
    result = total + jnp.dot(piece[1], imag_rows, preferred_element_type=jnp.float32)
    return jnp.stack([result[:, :cols_here], result[:, cols_here:]]).astype(jnp.bfloat16)


def solution(mesh):
    finer = Mesh(
        mesh.devices.reshape(2, 4, 2, mesh.shape["band"]), ("ga_0", "ga_1", "ga_2", "band")
    )
    return jax.shard_map(
        local,
        mesh=finer,
        in_specs=(P(None, GA, "band"), P(None, GA, "band")),
        out_specs=P(None, GA, "band"),
        check_vma=False,
    )
```

profile of v0, /device:TPU:225, one launch (start us, length us, event | category | flops | bytes accessed | tf_op | source)
XLA Modules:
  0.0 243.1 jit_solution(4615036172943029485)
XLA Ops:
  6.5 0.0 all-gather.2.cloned.1.call-start
  6.5 0.7 all-gather.2.cloned.1.call-update
  7.3 1.1 broadcast_in_dim.6
  8.4 196.2 %all_to_all.10 = bf16[8,2,256,256]{3,2,1,0:T(8,128)(2,1)S(1)} all-to-all(bf16[8,2,256,256]{3,2,1,0:T(8,128)(2,1)S(1)} %broadcast_in_dim.6), channel_id=1, replica_groups=mesh['ga_0'=2,'ga_1'=4,'ga_2'=2,'band'=16] {'ga_0','ga_1'}, dimensions={0} | all-to-all | bytes 4194304 | tf_op jit(solution)/shard_map/all_to_all | solution.py:12
  204.7 0.5 broadcast_in_dim.7
  205.1 9.2 %all_to_all.11 = bf16[2,8,2,256,256]{4,3,2,1,0:T(8,128)(2,1)S(1)} all-to-all(bf16[2,8,2,256,256]{4,3,2,1,0:T(8,128)(2,1)S(1)} %broadcast_in_dim.7), channel_id=1, replica_groups=mesh['ga_0'=2,'ga_1'=4,'ga_2'=2,'band'=16] {'ga_2'}, dimensions={0} | all-to-all | bytes 8388608 | tf_op jit(solution)/shard_map/all_to_all | solution.py:12
  214.3 0.4 copy.5
  214.7 1.6 fusion.15
  216.4 1.6 bitcast_negate_fusion
  217.9 0.0 all-gather.2.cloned.1.call-done
  217.9 0.0 copy-start
  217.9 8.9 %fusion = f32[512,1024]{1,0:T(8,128)S(1)} fusion(bf16[2,1024,4096]{2,1,0:T(8,128)(2,1)} %all-gather.2.cloned.1.call-done, bf16[4096,256]{1,0:T(8,128)(2,1)} %bitcast.26, bf16[4096,256]{1,0:T(8,128)(2,1)} %bitcast_negate_fusion), kind=kOutput, calls=%fused_computation.1 | convolution fusion | flops 4303355904 | bytes 14680064 | tf_op jit(solution)/shard_map/dot_general | solution.py:34
  226.8 0.0 copy-done
  226.8 8.0 %fusion.10 = bf16[1024,512]{0,1:T(8,128)(2,1)S(1)} fusion(f32[512,1024]{1,0:T(8,128)S(1)} %fusion, bf16[2,1024,4096]{2,1,0:T(8,128)(2,1)} %all-gather.2.cloned.1.call-done, bf16[4096,256]{1,0:T(8,128)(2,1)S(1)} %bitcast.25, bf16[4096,256]{1,0:T(8,128)(2,1)S(1)} %bitcast.27), kind=kOutput, calls=%fused_computation.11 | convolution fusion | flops 4304404480 | bytes 15728640 | tf_op jit(solution)/shard_map/dot_general | solution.py:33
  234.8 0.1 slice_bitcast_fusion.9
  234.9 0.1 pad_maximum_fusion
  235.0 1.3 copy.6
Async XLA Ops:
  6.5 211.4 %all-gather.2.cloned.1.call-start = ((), (), s32[]{:S(2)}) async-start(), calls=%async_computation.2 | async-start | bytes 17825792 | tf_op jit(solution)/shard_map/all_gather | solution.py:32
  217.9 8.9 %copy-start = (bf16[1,16,256,256]{3,2,0,1:T(8,128)(2,1)S(1)}, bf16[1,16,256,256]{3,2,0,1:T(8,128)(2,1)}, u32[]{:S(2)}) copy-start(bf16[1,16,256,256]{3,2,0,1:T(8,128)(2,1)} %get-tuple-element.6) | copy-start | bytes 6291460
Sparse Core Ops, SparseCore 0:
  9.0 189.7 all-gather.1
where the time goes:
time: 243 us
  blocking collectives  205 us (84%)
  matrix products  16.8 us (7%)
  between operations  13.5 us (6%)
  local copies, waits for them, and re-layouts  5.04 us (2%)
    all_to_all x2, blocking collectives, sent_to_all(): return lax.all_to_all(copies, axis, split_axis=0, concat_axis=0, tiled=True)  205 us
    dot_general x1, matrix products, local(): jnp.dot(piece[1], imag_rows, preferred_element_type=jnp.float32)  8.89 us
    dot_general x1, matrix products, local(): total = jnp.dot(piece[0], real_rows, preferred_element_type=jnp.float32)  7.95 us
  transfers between devices with their start and end apart: 1, of which 0 were waited for; matrix products, arithmetic and copies ran while one was open for 2% of the time, Pallas kernels for 0%

commit v1 on v0

v1 whole, which is shorter than its diff:
```python
import functools

import jax
import jax.numpy as jnp
from jax import lax
from jax.experimental import pallas as pl
from jax.experimental.pallas import tpu as pltpu
from jax.sharding import Mesh
from jax.sharding import PartitionSpec as P

GA = ("xh", "y", "core")
BAND = ("xl", "z")
MESH = pl.DeviceIdType.MESH

CHUNKS = (128, 128, 128, 64, 64)
STARTS = tuple(sum(CHUNKS[:i]) for i in range(len(CHUNKS)))
N = len(CHUNKS)
HALF = 512
W = 256
HOPS = ((4, 3), (3, 4))


def kernel(
    waves, rot, out,
    a, xs, b, cs, acc,
    load_sem, ax_send, ax_recv, az_send, az_recv,
    bx_send, bx_recv, by_send, by_recv, bs_send, bs_recv,
    c_send, c_recv, c_local,
):
    xh, y, core = lax.axis_index("xh"), lax.axis_index("y"), lax.axis_index("core")
    xl, z = lax.axis_index("xl"), lax.axis_index("z")
    x = xh * 2 + xl

    def at_x(dx):
        there = (x + dx + 4) % 4
        return {"xh": there // 2, "xl": there % 2}

    def at_y(dy):
        return {"y": (y + dy + 4) % 4}

    def at_z(dz):
        return {"z": (z + dz + 8) % 8}

    partner = {"xl": 1 - xl}
    sibling = {"core": 1 - core}

    def rows(i, base=0):
        return pl.ds(base + STARTS[i], CHUNKS[i])

    def piece(i, kb, dz):
        side = xl if kb == 0 else 1 - xl
        return a.at[side * 8 + (z + dz + 16) % 8, :, rows(i), :]

    def block(dx, dy, who=None):
        there = (x + dx + 4) % 4
        who = core if who is None else who
        return b.at[(there // 2) * 8 + ((y + dy + 4) % 4) * 2 + who, there % 2]

    def remote(src, dst, send, recv, where):
        return pltpu.make_async_remote_copy(
            src_ref=src, dst_ref=dst, send_sem=send, recv_sem=recv,
            device_id=where, device_id_type=MESH,
        )

    sent = []

    def go(src, dst, send, recv, where):
        copy = remote(src, dst, send, recv, where)
        copy.start()
        sent.append(copy)

    def arrived(dst, send, recv, where):
        remote(dst, dst, send, recv, where).wait_recv()

    def load_own(i):
        return pltpu.make_async_copy(
            waves.at[:, rows(i, xl * HALF), :], piece(i, 0, 0), load_sem.at[0, i])

    def load_other(i):
        return pltpu.make_async_copy(
            waves.at[:, rows(i, (1 - xl) * HALF), :], xs.at[:, rows(i), :], load_sem.at[1, i])

    load_rot = pltpu.make_async_copy(rot, block(0, 0), load_sem.at[0, N])

    load_own(0).start()
    load_other(0).start()
    load_rot.start()
    for i in range(1, N):
        load_own(i).start()
        load_other(i).start()

    barrier = pltpu.get_barrier_semaphore()
    for where in (at_x(1), at_x(-1), at_y(1), at_y(-1), at_z(1), at_z(-1), sibling):
        pl.semaphore_signal(barrier, inc=1, device_id=where, device_id_type=MESH)
    pl.semaphore_wait(barrier, 7)

    def swap(i):
        load_other(i).wait()
        go(xs.at[:, rows(i), :], piece(i, 0, 0), ax_send.at[i], ax_recv.at[i], partner)

    def slot(kb, d, t):
        return (kb * 2 + d) * 4 + t

    def ring(i, kb, d, t):
        s = slot(kb, d, t)
        ref = piece(i, kb, -t if d == 0 else t)
        go(ref, ref, az_send.at[i, s], az_recv.at[i, s], at_z(1 if d == 0 else -1))

    def own(i, kb):
        if kb == 0:
            load_own(i).wait()
        else:
            arrived(piece(i, 1, 0), ax_send.at[i], ax_recv.at[i], partner)
        ring(i, kb, 0, 0)
        ring(i, kb, 1, 0)

    def step(i, t):
        for kb in range(2):
            for d in range(2):
                if t <= HOPS[kb][d]:
                    s = slot(kb, d, t - 1)
                    arrived(piece(i, kb, -t if d == 0 else t), az_send.at[i, s],
                            az_recv.at[i, s], at_z(1 if d == 0 else -1))
                    if t < HOPS[kb][d]:
                        ring(i, kb, d, t)

    COLS = (0, -1, 1, 2)

    def to_sibling(j, k):
        ref = block(COLS[j], (0, -1, 1, 2)[k])
        go(ref, ref, bs_send.at[j, k], bs_recv.at[j, k], sibling)

    def to_y(j):
        ref = block(COLS[j], 0)
        go(ref, ref, by_send.at[j, 0], by_recv.at[j, 0], at_y(1))
        go(ref, ref, by_send.at[j, 1], by_recv.at[j, 1], at_y(-1))
        to_sibling(j, 0)

    def b_start():
        load_rot.wait()
        ref = block(0, 0)
        go(ref, ref, bx_send.at[0], bx_recv.at[0], at_x(1))
        go(ref, ref, bx_send.at[1], bx_recv.at[1], at_x(-1))
        to_y(0)

    def b_x1():
        for d, dx in ((0, -1), (1, 1)):
            ref = block(dx, 0)
            arrived(ref, bx_send.at[d], bx_recv.at[d], at_x(-dx))
            part = ref.at[d]
            go(part, part, bx_send.at[2 + d], bx_recv.at[2 + d], at_x(-dx))
            to_y(1 + d)

    def b_x2():
        for d, dx in ((0, -2), (1, 2)):
            arrived(block(2, 0).at[d], bx_send.at[2 + d], bx_recv.at[2 + d], at_x(1 - 2 * d))
        to_y(3)

    def b_y1(j):
        for d, dy in ((0, -1), (1, 1)):
            ref = block(COLS[j], dy)
            arrived(ref, by_send.at[j, d], by_recv.at[j, d], at_y(-dy))
            part = ref.at[d]
            go(part, part, by_send.at[j, 2 + d], by_recv.at[j, 2 + d], at_y(-dy))
            to_sibling(j, 1 + d)

    def b_y2(j):
        for d in range(2):
            arrived(block(COLS[j], 2).at[d], by_send.at[j, 2 + d], by_recv.at[j, 2 + d],
                    at_y(1 - 2 * d))
        to_sibling(j, 3)

    def b_sibling():
        for j in range(4):
            for k in range(4):
                arrived(block(COLS[j], (0, -1, 1, 2)[k], 1 - core),
                        bs_send.at[j, k], bs_recv.at[j, k], sibling)

    def compute(i, low, high):
        r = CHUNKS[i]
        if low == 0:
            acc[:, : 2 * r, :] = jnp.zeros((2, 2 * r, 2 * W), jnp.float32)

        def body(m, carry):
            dz = ((m + 1) // 2) * (1 - 2 * (m % 2))
            place = (z + dz + 8) % 8
            lhs = [
                a[side * 8 + place, :, rows(i), :].reshape(2 * r, W) for side in (0, 1)
            ]
            for n in range(2):
                which = 1 - xl if n == 0 else xl
                for cd in range(2):
                    total = acc[n, : 2 * r, cd * W : (cd + 1) * W]
                    for side in (0, 1):
                        total = total + jnp.dot(
                            lhs[side], b[side * 8 + place, which, cd],
                            preferred_element_type=jnp.float32)
                    acc[n, : 2 * r, cd * W : (cd + 1) * W] = total
            return carry

        lax.fori_loop(low, high, body, 0)

    def store_own(i):
        return pltpu.make_async_copy(
            cs.at[1, :, rows(i), :], out.at[:, rows(i, xl * HALF), :], c_local.at[i])

    def finish(i):
        r = CHUNKS[i]
        for n in range(2):
            cs[n, 0, rows(i), :] = (acc[n, :r, :W] - acc[n, r : 2 * r, W:]).astype(jnp.bfloat16)
            cs[n, 1, rows(i), :] = (acc[n, :r, W:] + acc[n, r : 2 * r, :W]).astype(jnp.bfloat16)
        go(cs.at[0, :, rows(i), :], out.at[:, rows(i, xl * HALF), :],
           c_send.at[i], c_recv.at[i], partner)
        store_own(i).start()

    own(0, 0)
    swap(0)
    b_start()
    swap(1)
    own(1, 0)
    own(0, 1)
    for i in range(2, N):
        swap(i)
    own(1, 1)
    step(0, 1)
    b_y1(0)
    b_x1()
    step(0, 2)
    b_x2()
    step(0, 3)
    b_y1(1)
    b_y1(2)
    own(2, 0)
    own(2, 1)
    step(1, 1)
    b_y1(3)
    step(0, 4)
    step(1, 2)
    b_y2(0)
    b_y2(1)
    b_y2(2)
    step(1, 3)
    b_y2(3)
    b_sibling()
    own(3, 0)
    own(3, 1)
    step(2, 1)
    compute(0, 0, 4)
    step(2, 2)
    compute(0, 4, 8)
    finish(0)
    step(1, 4)
    step(2, 3)
    own(4, 0)
    own(4, 1)
    compute(1, 0, 4)
    step(3, 1)
    compute(1, 4, 8)
    finish(1)
    step(3, 2)
    step(2, 4)
    compute(2, 0, 4)
    step(3, 3)
    compute(2, 4, 8)
    step(4, 1)
    finish(2)
    step(4, 2)
    step(3, 4)
    compute(3, 0, 4)
    step(4, 3)
    compute(3, 4, 8)
    finish(3)
    compute(4, 0, 7)
    step(4, 4)
    compute(4, 7, 8)
    finish(4)

    for copy in sent:
        copy.wait_send()
    for i in range(N):
        store_own(i).wait()
        arrived(out.at[:, rows(i, (1 - xl) * HALF), :], c_send.at[i], c_recv.at[i], partner)


def local(waves, rotation):
    dma = pltpu.SemaphoreType.DMA
    return pl.pallas_call(
        kernel,
        out_shape=jax.ShapeDtypeStruct(waves.shape, waves.dtype),
        in_specs=[pl.BlockSpec(memory_space=pl.ANY)] * 2,
        out_specs=pl.BlockSpec(memory_space=pl.ANY),
        scratch_shapes=[
            pltpu.VMEM((16, 2, HALF, W), jnp.bfloat16),
            pltpu.VMEM((2, HALF, W), jnp.bfloat16),
            pltpu.VMEM((16, 2, 2, W, W), jnp.bfloat16),
            pltpu.VMEM((2, 2, HALF, W), jnp.bfloat16),
            pltpu.VMEM((2, 2 * max(CHUNKS), 2 * W), jnp.float32),
            dma((2, N + 1)),
            dma((N,)), dma((N,)),
            dma((N, 16)), dma((N, 16)),
            dma((4,)), dma((4,)),
            dma((4, 4)), dma((4, 4)),
            dma((4, 4)), dma((4, 4)),
            dma((N,)), dma((N,)), dma((N,)),
        ],
        compiler_params=pltpu.CompilerParams(
            collective_id=0, has_side_effects=True, vmem_limit_bytes=60 * 1024 * 1024),
        name="rotate",
    )(waves, rotation)


def solution(mesh):
    finer = Mesh(
        mesh.devices.reshape(2, 4, 2, 2, 8), ("xh", "y", "core", "xl", "z")
    )
    return jax.shard_map(
        local,
        mesh=finer,
        in_specs=(P(None, GA, BAND), P(None, GA, BAND)),
        out_specs=P(None, GA, BAND),
        check_vma=False,
    )
```

time: 243 us -> 113 us (0.47)
  the two profiles are of different devices: /device:TPU:225 before, /device:TPU:4 now
where the time goes in v1:
time: 113 us; the launch traced here: 112 us
  Pallas kernels  110 us (97%)
  local copies, waits for them, and re-layouts  2.26 us (2%)
    pallas_call x1, Pallas kernels, local(): pl.pallas_call(kernel, out_shape=jax.ShapeDtypeStruct(waves.shape, waves....  110 us
    unnamed x1, local copies, waits for them, and re-layouts  2.26 us

profile of v1, /device:TPU:4, one launch (start us, length us, event | category | flops | bytes accessed | tf_op | source)
XLA Modules:
  0.0 112.4 jit_solution(18372338870586142884)
XLA Ops:
  0.0 110.1 %rotate.1 = bf16[2,1024,256]{2,1,0:T(8,128)(2,1)} custom-call(bf16[2,1024,256]{2,1,0:T(8,128)(2,1)} %waves.1, bf16[2,256,256]{2,1,0:T(8,128)(2,1)} %rot.1), custom_call_target="tpu_custom_call" | custom-call | tf_op jit(solution)/shard_map/rotate/pallas_call | solution.py:287
  110.1 2.3 %copy.4 = bf16[2,1024,256]{2,1,0:T(8,128)(2,1)} copy(bf16[2,1024,256]{2,1,0:T(8,128)(2,1)} %rotate.1) | data formatting | bytes 2097152

commit v2 on v0

v2 whole, which is shorter than its diff:
```python
import jax
import jax.numpy as jnp
from jax import lax
from jax.experimental import pallas as pl
from jax.experimental.pallas import tpu as pltpu
from jax.sharding import Mesh
from jax.sharding import PartitionSpec as P

GA = ("xh", "y", "core")
BAND = ("xl", "z")
MESH = pl.DeviceIdType.MESH

CHUNKS = (128, 64, 64)
STARTS = tuple(sum(CHUNKS[:i]) for i in range(len(CHUNKS)))
N = len(CHUNKS)
HALF = 512
QUARTER = 256
W = 256
NEAR = (0, -1, 1, 2)


def kernel(
    waves, rot, out,
    a, u, via, xs, b, cs, acc,
    load_sem, ax_send, ax_recv, az_send, az_recv,
    bz_send, bz_recv, b1_send, b1_recv, b2_send, b2_recv, bs_send, bs_recv,
    c_send, c_recv, c_local,
):
    xh, y, core = lax.axis_index("xh"), lax.axis_index("y"), lax.axis_index("core")
    xl, z = lax.axis_index("xl"), lax.axis_index("z")
    x = xh * 2 + xl
    s = 1 - 2 * (z % 2)
    kind = (z // 2) % 2

    def plane(d):
        return (z + s * d + 8) % 8

    def at_x(dx):
        there = (x + dx + 4) % 4
        return {"xh": there // 2, "xl": there % 2}

    def at_y(dy):
        return {"y": (y + dy + 4) % 4}

    inner = {"z": plane(1)}
    outer = {"z": plane(-1)}
    partner = {"xl": 1 - xl}
    across = {"xl": 1 - xl, "z": plane(-1)}
    sibling = {"core": 1 - core}

    def rows(i, base=0):
        return pl.ds(base + STARTS[i], CHUNKS[i])

    def remote(src, dst, send, recv, where):
        return pltpu.make_async_remote_copy(
            src_ref=src, dst_ref=dst, send_sem=send, recv_sem=recv,
            device_id=where, device_id_type=MESH,
        )

    sent = []

    def go(src, dst, send, recv, where):
        copy = remote(src, dst, send, recv, where)
        copy.start()
        sent.append(copy)

    def arrived(dst, send, recv, where):
        remote(dst, dst, send, recv, where).wait_recv()

    def mine(i, kb, d):
        side = xl if kb == 0 else 1 - xl
        return a.at[side * 8 + plane(d), :, rows(i), :]

    def theirs(i, kb):
        return u.at[kb, :, rows(i), :]

    def passing(i, kb, j):
        return via.at[j, kb, :, rows(i), :]

    def spare(i, j):
        return xs.at[j, :, rows(i), :]

    def load(i, j):
        half = xl if j < 2 else 1 - xl
        quarter = kind if j % 2 == 0 else 1 - kind
        dst = (mine(i, 0, 0), theirs(i, 0), spare(i, 0), spare(i, 1))[j]
        return pltpu.make_async_copy(
            waves.at[:, rows(i, half * HALF + quarter * QUARTER), :], dst, load_sem.at[j, i])

    def swap(i):
        load(i, 2).wait()
        go(spare(i, 0), mine(i, 0, 0), ax_send.at[0, i], ax_recv.at[0, i], partner)
        load(i, 3).wait()
        go(spare(i, 1), theirs(i, 1), ax_send.at[1, i], ax_recv.at[1, i], partner)

    def landing(i, kb, n):
        if n == 1:
            return passing(i, kb, 0)
        if n == 5:
            return passing(i, kb, 1)
        if n == 6:
            return passing(i, kb, 2)
        return mine(i, kb, {0: -1, 2: -2, 3: -3, 4: 1, 7: 2, 8: 3, 9: 4}[n])

    def over(i, kb, n, src, dst):
        k = kb * 10 + n
        go(src, dst, az_send.at[i, k], az_recv.at[i, k], outer if n < 4 else inner)

    def wait(i, kb, n):
        k = kb * 10 + n
        arrived(landing(i, kb, n), az_send.at[i, k], az_recv.at[i, k], outer if n < 4 else inner)

    def pass_on(i, kb, got, n):
        wait(i, kb, got)
        src = landing(i, kb, got)
        over(i, kb, n, src, passing(i, kb, 2) if n == 6 else src if got != 5 and got != 6 else
             mine(i, kb, 1 if got == 5 else 2))

    def own(i, kb):
        if kb == 0:
            load(i, 0).wait()
            load(i, 1).wait()
        else:
            arrived(mine(i, 1, 0), ax_send.at[0, i], ax_recv.at[0, i], partner)
            arrived(theirs(i, 1), ax_send.at[1, i], ax_recv.at[1, i], partner)
        over(i, kb, 5, theirs(i, kb), passing(i, kb, 1))
        over(i, kb, 1, mine(i, kb, 0), passing(i, kb, 0))
        over(i, kb, 4, mine(i, kb, 0), mine(i, kb, 0))
        over(i, kb, 0, theirs(i, kb), mine(i, kb, 0))

    def step(i, t):
        for kb in range(2):
            if t == 1:
                pass_on(i, kb, 1, 6)
                pass_on(i, kb, 5, 2)
                pass_on(i, kb, 0, 7)
            elif t == 2:
                pass_on(i, kb, 6, 3)
                pass_on(i, kb, 2, 8)
            elif t == 3:
                pass_on(i, kb, 3, 9)
            elif t == 4:
                wait(i, kb, 4)
                wait(i, kb, 7)
                wait(i, kb, 8)
            else:
                wait(i, kb, 9)

    def first(g, d):
        return at_x(d) if g == 0 else at_y(d)

    def second(g, d):
        return at_y(d) if g == 0 else at_x(d)

    def block(g, d1, d2, who=None):
        dx, dy = (d1, d2) if g == 0 else (d2, d1)
        there = (x + dx + 4) % 4
        who = core if who is None else who
        return b.at[g, (there // 2) * 8 + ((y + dy + 4) % 4) * 2 + who, there % 2]

    load_rot = pltpu.make_async_copy(rot, block(0, 0, 0), load_sem.at[0, N])

    def to_sibling(g, j, k):
        ref = block(g, NEAR[j], NEAR[k])
        go(ref, ref, bs_send.at[g, j * 4 + k], bs_recv.at[g, j * 4 + k], sibling)

    def to_second(g, j):
        ref = block(g, NEAR[j], 0)
        for d in range(2):
            n = j * 4 + d
            go(ref, ref, b2_send.at[g, n], b2_recv.at[g, n], second(g, 1 - 2 * d))
        to_sibling(g, j, 0)

    def b_out():
        load_rot.wait()
        go(block(0, 0, 0), block(1, 0, 0), bz_send, bz_recv, outer)

    def b_start(g):
        ref = block(g, 0, 0)
        if g == 1:
            arrived(ref, bz_send, bz_recv, outer)
        for d in range(2):
            go(ref, ref, b1_send.at[g, d], b1_recv.at[g, d], first(g, 1 - 2 * d))
        to_second(g, 0)

    def b_first(g):
        for d in range(2):
            ref = block(g, 2 * d - 1, 0)
            arrived(ref, b1_send.at[g, d], b1_recv.at[g, d], first(g, 1 - 2 * d))
            part = ref.at[d]
            go(part, part, b1_send.at[g, 2 + d], b1_recv.at[g, 2 + d], first(g, 1 - 2 * d))
            to_second(g, 1 + d)

    def b_far(g):
        for d in range(2):
            arrived(block(g, 2, 0).at[d], b1_send.at[g, 2 + d], b1_recv.at[g, 2 + d],
                    first(g, 1 - 2 * d))
        to_second(g, 3)

    def b_second(g, j):
        for d in range(2):
            n = j * 4 + d
            ref = block(g, NEAR[j], 2 * d - 1)
            arrived(ref, b2_send.at[g, n], b2_recv.at[g, n], second(g, 1 - 2 * d))
            part = ref.at[d]
            go(part, part, b2_send.at[g, n + 2], b2_recv.at[g, n + 2], second(g, 1 - 2 * d))
            to_sibling(g, j, 1 + d)

    def b_last(g, j):
        for d in range(2):
            n = j * 4 + 2 + d
            arrived(block(g, NEAR[j], 2).at[d], b2_send.at[g, n], b2_recv.at[g, n],
                    second(g, 1 - 2 * d))
        to_sibling(g, j, 3)

    def b_sibling(g):
        for j in range(4):
            for k in range(4):
                arrived(block(g, NEAR[j], NEAR[k], 1 - core),
                        bs_send.at[g, j * 4 + k], bs_recv.at[g, j * 4 + k], sibling)

    def compute(i, low, high):
        r = CHUNKS[i]
        if low == 0:
            acc[:, : 2 * r, :] = jnp.zeros((4, 2 * r, 2 * W), jnp.float32)

        def body(m, carry):
            place = plane(((m + 1) // 2) * (2 * (m % 2) - 1))
            lhs = [
                a[side * 8 + place, :, rows(i), :].reshape(2 * r, W) for side in (0, 1)
            ]
            for g in range(2):
                for n in range(2):
                    which = xl if n == 0 else 1 - xl
                    for cd in range(2):
                        total = acc[g * 2 + n, : 2 * r, cd * W : (cd + 1) * W]
                        for side in (0, 1):
                            total = total + jnp.dot(
                                lhs[side], b[g, side * 8 + place, which, cd],
                                preferred_element_type=jnp.float32)
                        acc[g * 2 + n, : 2 * r, cd * W : (cd + 1) * W] = total
            return carry

        lax.fori_loop(low, high, body, 0)

    def out_rows(i, half, quarter):
        return out.at[:, rows(i, half * HALF + quarter * QUARTER), :]

    def store_own(i):
        return pltpu.make_async_copy(
            cs.at[0, :, rows(i), :], out_rows(i, xl, kind), c_local.at[i])

    AWAY = ((3, across), (2, outer), (1, partner))

    def finish(i):
        r = CHUNKS[i]
        for n in (3, 2, 1, 0):
            cs[n, 0, rows(i), :] = (acc[n, :r, :W] - acc[n, r : 2 * r, W:]).astype(jnp.bfloat16)
            cs[n, 1, rows(i), :] = (acc[n, :r, W:] + acc[n, r : 2 * r, :W]).astype(jnp.bfloat16)
        for n, where in AWAY:
            go(cs.at[n, :, rows(i), :], out_rows(i, xl, kind), c_send.at[n, i], c_recv.at[n, i], where)
        store_own(i).start()

    for i in range(N):
        load(i, 0).start()
        load(i, 1).start()
        load(i, 2).start()
        load(i, 3).start()
        if i == 0:
            load_rot.start()

    barrier = pltpu.get_barrier_semaphore()
    for where in (at_x(1), at_x(-1), at_y(1), at_y(-1), inner, outer, across, sibling):
        pl.semaphore_signal(barrier, inc=1, device_id=where, device_id_type=MESH)
    pl.semaphore_wait(barrier, 8)

    own(0, 0)
    swap(0)
    b_out()
    b_start(0)
    own(1, 0)
    swap(1)
    swap(2)
    own(0, 1)
    own(2, 0)
    b_start(1)
    step(0, 1)
    b_second(0, 0)
    own(1, 1)
    b_first(0)
    step(1, 1)
    step(0, 2)
    own(2, 1)
    b_far(0)
    b_first(1)
    step(2, 1)
    b_second(1, 0)
    b_second(0, 1)
    step(1, 2)
    step(0, 3)
    b_second(0, 2)
    b_far(1)
    b_second(1, 1)
    step(2, 2)
    step(1, 3)
    b_second(0, 3)
    b_second(1, 2)
    step(2, 3)
    b_last(0, 0)
    b_last(1, 0)
    b_second(1, 3)
    b_last(0, 1)
    b_last(0, 2)
    b_last(1, 1)
    b_last(1, 2)
    b_last(0, 3)
    b_last(1, 3)
    step(0, 4)
    step(0, 5)
    b_sibling(0)
    b_sibling(1)
    compute(0, 0, 8)
    finish(0)
    step(1, 4)
    step(1, 5)
    compute(1, 0, 8)
    finish(1)
    step(2, 4)
    compute(2, 0, 7)
    step(2, 5)
    compute(2, 7, 8)
    finish(2)

    for copy in sent:
        copy.wait_send()
    for i in range(N):
        store_own(i).wait()
        for n, where in AWAY:
            half = xl if n == 2 else 1 - xl
            quarter = kind if n == 1 else 1 - kind
            arrived(out_rows(i, half, quarter), c_send.at[n, i], c_recv.at[n, i], where)


def local(waves, rotation):
    dma = pltpu.SemaphoreType.DMA
    bf16 = jnp.bfloat16
    return pl.pallas_call(
        kernel,
        out_shape=jax.ShapeDtypeStruct(waves.shape, waves.dtype),
        in_specs=[pl.BlockSpec(memory_space=pl.ANY)] * 2,
        out_specs=pl.BlockSpec(memory_space=pl.ANY),
        scratch_shapes=[
            pltpu.VMEM((16, 2, QUARTER, W), bf16),
            pltpu.VMEM((2, 2, QUARTER, W), bf16),
            pltpu.VMEM((3, 2, 2, QUARTER, W), bf16),
            pltpu.VMEM((2, 2, QUARTER, W), bf16),
            pltpu.VMEM((2, 16, 2, 2, W, W), bf16),
            pltpu.VMEM((4, 2, QUARTER, W), bf16),
            pltpu.VMEM((4, 2 * max(CHUNKS), 2 * W), jnp.float32),
            dma((4, N + 1)),
            dma((2, N)), dma((2, N)),
            dma((N, 20)), dma((N, 20)),
            dma, dma,
            dma((2, 4)), dma((2, 4)),
            dma((2, 16)), dma((2, 16)),
            dma((2, 16)), dma((2, 16)),
            dma((4, N)), dma((4, N)), dma((N,)),
        ],
        compiler_params=pltpu.CompilerParams(
            collective_id=0, has_side_effects=True, vmem_limit_bytes=60 * 1024 * 1024),
        name="rotate",
    )(waves, rotation)


def solution(mesh):
    finer = Mesh(
        mesh.devices.reshape(2, 4, 2, 2, 8), ("xh", "y", "core", "xl", "z")
    )
    return jax.shard_map(
        local,
        mesh=finer,
        in_specs=(P(None, GA, BAND), P(None, GA, BAND)),
        out_specs=P(None, GA, BAND),
        check_vma=False,
    )
```

time: 243 us -> 98.4 us (0.40)
  the two profiles are of different devices: /device:TPU:225 before, /device:TPU:1 now
where the time goes in v2:
time: 98.4 us; the launch traced here: 98.2 us
  Pallas kernels  96 us (98%)
  local copies, waits for them, and re-layouts  2.26 us (2%)
    pallas_call x1, Pallas kernels, local(): pl.pallas_call(kernel, out_shape=jax.ShapeDtypeStruct(waves.shape, waves....  96 us
    unnamed x1, local copies, waits for them, and re-layouts  2.26 us

profile of v2, /device:TPU:1, one launch (start us, length us, event | category | flops | bytes accessed | tf_op | source)
XLA Modules:
  0.0 98.2 jit_solution(11162587229176422629)
XLA Ops:
  0.0 96.0 %rotate.1 = bf16[2,1024,256]{2,1,0:T(8,128)(2,1)} custom-call(bf16[2,1024,256]{2,1,0:T(8,128)(2,1)} %waves.1, bf16[2,256,256]{2,1,0:T(8,128)(2,1)} %rot.1), custom_call_target="tpu_custom_call" | custom-call | tf_op jit(solution)/shard_map/rotate/pallas_call | solution.py:347
  96.0 2.3 %copy.4 = bf16[2,1024,256]{2,1,0:T(8,128)(2,1)} copy(bf16[2,1024,256]{2,1,0:T(8,128)(2,1)} %rotate.1) | data formatting | bytes 2097152

commit v3 on v2

--- a/solution.py
+++ b/solution.py
@@ -10,7 +10,8 @@
 BAND = ("xl", "z")
 MESH = pl.DeviceIdType.MESH
 
-CHUNKS = (128, 64, 64)
+CHUNKS = (96, 96, 64)
+PARTS = ((0, 96), (96, 96), (192, 64))
 STARTS = tuple(sum(CHUNKS[:i]) for i in range(len(CHUNKS)))
 N = len(CHUNKS)
 HALF = 512
@@ -24,7 +25,7 @@
     a, u, via, xs, b, cs, acc,
     load_sem, ax_send, ax_recv, az_send, az_recv,
     bz_send, bz_recv, b1_send, b1_recv, b2_send, b2_recv, bs_send, bs_recv,
-    c_send, c_recv, c_local,
+    c_send, c_recv,
 ):
     xh, y, core = lax.axis_index("xh"), lax.axis_index("y"), lax.axis_index("core")
     xl, z = lax.axis_index("xl"), lax.axis_index("z")
@@ -128,24 +129,6 @@
         over(i, kb, 4, mine(i, kb, 0), mine(i, kb, 0))
         over(i, kb, 0, theirs(i, kb), mine(i, kb, 0))
 
-    def step(i, t):
-        for kb in range(2):
-            if t == 1:
-                pass_on(i, kb, 1, 6)
-                pass_on(i, kb, 5, 2)
-                pass_on(i, kb, 0, 7)
-            elif t == 2:
-                pass_on(i, kb, 6, 3)
-                pass_on(i, kb, 2, 8)
-            elif t == 3:
-                pass_on(i, kb, 3, 9)
-            elif t == 4:
-                wait(i, kb, 4)
-                wait(i, kb, 7)
-                wait(i, kb, 8)
-            else:
-                wait(i, kb, 9)
-
     def first(g, d):
         return at_x(d) if g == 0 else at_y(d)
 
@@ -183,13 +166,12 @@
             go(ref, ref, b1_send.at[g, d], b1_recv.at[g, d], first(g, 1 - 2 * d))
         to_second(g, 0)
 
-    def b_first(g):
-        for d in range(2):
-            ref = block(g, 2 * d - 1, 0)
-            arrived(ref, b1_send.at[g, d], b1_recv.at[g, d], first(g, 1 - 2 * d))
-            part = ref.at[d]
-            go(part, part, b1_send.at[g, 2 + d], b1_recv.at[g, 2 + d], first(g, 1 - 2 * d))
-            to_second(g, 1 + d)
+    def b_first(g, d):
+        ref = block(g, 2 * d - 1, 0)
+        arrived(ref, b1_send.at[g, d], b1_recv.at[g, d], first(g, 1 - 2 * d))
+        part = ref.at[d]
+        go(part, part, b1_send.at[g, 2 + d], b1_recv.at[g, 2 + d], first(g, 1 - 2 * d))
+        to_second(g, 1 + d)
 
     def b_far(g):
         for d in range(2):
@@ -197,14 +179,13 @@
                     first(g, 1 - 2 * d))
         to_second(g, 3)
 
-    def b_second(g, j):
-        for d in range(2):
-            n = j * 4 + d
-            ref = block(g, NEAR[j], 2 * d - 1)
-            arrived(ref, b2_send.at[g, n], b2_recv.at[g, n], second(g, 1 - 2 * d))
-            part = ref.at[d]
-            go(part, part, b2_send.at[g, n + 2], b2_recv.at[g, n + 2], second(g, 1 - 2 * d))
-            to_sibling(g, j, 1 + d)
+    def b_second(g, j, d):
+        n = j * 4 + d
+        ref = block(g, NEAR[j], 2 * d - 1)
+        arrived(ref, b2_send.at[g, n], b2_recv.at[g, n], second(g, 1 - 2 * d))
+        part = ref.at[d]
+        go(part, part, b2_send.at[g, n + 2], b2_recv.at[g, n + 2], second(g, 1 - 2 * d))
+        to_sibling(g, j, 1 + d)
 
     def b_last(g, j):
         for d in range(2):
@@ -219,47 +200,49 @@
                 arrived(block(g, NEAR[j], NEAR[k], 1 - core),
                         bs_send.at[g, j * 4 + k], bs_recv.at[g, j * 4 + k], sibling)
 
-    def compute(i, low, high):
-        r = CHUNKS[i]
+    def compute(p, g, low, high):
+        base, r = PARTS[p]
+        here = pl.ds(base, r)
         if low == 0:
-            acc[:, : 2 * r, :] = jnp.zeros((4, 2 * r, 2 * W), jnp.float32)
+            acc[2 * g : 2 * g + 2, pl.ds(2 * base, 2 * r), :] = jnp.zeros((2, 2 * r, 2 * W), jnp.float32)
 
         def body(m, carry):
             place = plane(((m + 1) // 2) * (2 * (m % 2) - 1))
-            lhs = [
-                a[side * 8 + place, :, rows(i), :].reshape(2 * r, W) for side in (0, 1)
-            ]
-            for g in range(2):
-                for n in range(2):
-                    which = xl if n == 0 else 1 - xl
-                    for cd in range(2):
-                        total = acc[g * 2 + n, : 2 * r, cd * W : (cd + 1) * W]
-                        for side in (0, 1):
-                            total = total + jnp.dot(
-                                lhs[side], b[g, side * 8 + place, which, cd],
-                                preferred_element_type=jnp.float32)
-                        acc[g * 2 + n, : 2 * r, cd * W : (cd + 1) * W] = total
+            lhs = [a[side * 8 + place, :, here, :].reshape(2 * r, W) for side in (0, 1)]
+            for n in range(2):
+                which = xl if n == 0 else 1 - xl
+                for cd in range(2):
+                    total = acc[g * 2 + n, pl.ds(2 * base, 2 * r), cd * W : (cd + 1) * W]
+                    for side in (0, 1):
+                        total = total + jnp.dot(
+                            lhs[side], b[g, side * 8 + place, which, cd],
+                            preferred_element_type=jnp.float32)
+                    acc[g * 2 + n, pl.ds(2 * base, 2 * r), cd * W : (cd + 1) * W] = total
             return carry
 
-        lax.fori_loop(low, high, body, 0)
-
-    def out_rows(i, half, quarter):
-        return out.at[:, rows(i, half * HALF + quarter * QUARTER), :]
-
-    def store_own(i):
-        return pltpu.make_async_copy(
-            cs.at[0, :, rows(i), :], out_rows(i, xl, kind), c_local.at[i])
+        lax.fori_loop(low, high, body, 0, unroll=high - low)
+
+    def out_rows(p, half, quarter):
+        base, r = PARTS[p]
+        return out.at[:, pl.ds(base + half * HALF + quarter * QUARTER, r), :]
+
+    def result(n, p):
+        base, r = PARTS[p]
+        return cs.at[n, :, pl.ds(base, r), :]
 
     AWAY = ((3, across), (2, outer), (1, partner))
 
-    def finish(i):
-        r = CHUNKS[i]
-        for n in (3, 2, 1, 0):
-            cs[n, 0, rows(i), :] = (acc[n, :r, :W] - acc[n, r : 2 * r, W:]).astype(jnp.bfloat16)
-            cs[n, 1, rows(i), :] = (acc[n, :r, W:] + acc[n, r : 2 * r, :W]).astype(jnp.bfloat16)
+    def finish(p, g):
+        base, r = PARTS[p]
+        here = pl.ds(base, r)
+        for n in (2 * g + 1, 2 * g):
+            top, low = pl.ds(2 * base, r), pl.ds(2 * base + r, r)
+            dst = out_rows(p, xl, kind) if n == 0 else result(n, p)
+            dst[0] = (acc[n, top, :W] - acc[n, low, W:]).astype(jnp.bfloat16)
+            dst[1] = (acc[n, top, W:] + acc[n, low, :W]).astype(jnp.bfloat16)
         for n, where in AWAY:
-            go(cs.at[n, :, rows(i), :], out_rows(i, xl, kind), c_send.at[n, i], c_recv.at[n, i], where)
-        store_own(i).start()
+            if n // 2 == g:
+                go(result(n, p), out_rows(p, xl, kind), c_send.at[n, p], c_recv.at[n, p], where)
 
     for i in range(N):
         load(i, 0).start()
@@ -274,71 +257,142 @@
         pl.semaphore_signal(barrier, inc=1, device_id=where, device_id_type=MESH)
     pl.semaphore_wait(barrier, 8)
 
-    own(0, 0)
-    swap(0)
     b_out()
     b_start(0)
-    own(1, 0)
+    swap(0)
+    own(0, 0)
     swap(1)
     swap(2)
-    own(0, 1)
+    own(1, 0)
+    pass_on(0, 0, 5, 2)
     own(2, 0)
     b_start(1)
-    step(0, 1)
-    b_second(0, 0)
+    b_second(0, 0, 0)
+    b_second(0, 0, 1)
+    b_first(0, 0)
+    b_first(0, 1)
+    pass_on(1, 0, 5, 2)
+    pass_on(0, 0, 1, 6)
+    pass_on(0, 0, 0, 7)
+    pass_on(2, 0, 5, 2)
+    own(0, 1)
+    pass_on(1, 0, 1, 6)
+    b_first(1, 0)
+    b_first(1, 1)
+    pass_on(0, 0, 6, 3)
+    pass_on(1, 0, 0, 7)
+    pass_on(0, 0, 2, 8)
+    b_last(0, 0)
+    pass_on(2, 0, 1, 6)
+    pass_on(0, 1, 5, 2)
+    pass_on(2, 0, 0, 7)
+    pass_on(1, 0, 2, 8)
+    b_second(0, 1, 0)
+    b_second(0, 1, 1)
+    pass_on(1, 0, 6, 3)
+    pass_on(2, 0, 2, 8)
+    b_second(1, 0, 0)
+    b_second(1, 0, 1)
+    pass_on(0, 1, 1, 6)
+    b_far(0)
+    pass_on(0, 1, 0, 7)
+    b_second(0, 2, 0)
+    b_second(0, 2, 1)
+    pass_on(2, 0, 6, 3)
+    pass_on(0, 0, 3, 9)
+    b_far(1)
+    pass_on(0, 1, 2, 8)
+    b_second(1, 1, 0)
+    b_second(1, 1, 1)
+    pass_on(1, 0, 3, 9)
+    b_last(0, 1)
+    pass_on(2, 0, 3, 9)
+    pass_on(0, 1, 6, 3)
+    b_second(1, 2, 0)
+    b_second(1, 2, 1)
+    b_second(0, 3, 0)
+    b_second(0, 3, 1)
+    pass_on(0, 1, 3, 9)
+    b_last(1, 0)
+    b_last(0, 2)
     own(1, 1)
-    b_first(0)
-    step(1, 1)
-    step(0, 2)
+    b_last(0, 3)
+    b_second(1, 3, 0)
+    b_second(1, 3, 1)
+    b_sibling(0)
+    wait(0, 0, 4)
+    wait(0, 1, 4)
+    wait(0, 0, 7)
+    wait(0, 1, 7)
+    compute(0, 0, 0, 4)
+    pass_on(1, 1, 1, 6)
+    wait(0, 0, 8)
+    wait(0, 1, 8)
+    compute(0, 0, 4, 7)
+    wait(0, 0, 9)
+    wait(0, 1, 9)
+    compute(0, 0, 7, 8)
+    finish(0, 0)
+    b_last(1, 1)
+    pass_on(1, 1, 5, 2)
     own(2, 1)
-    b_far(0)
-    b_first(1)
-    step(2, 1)
-    b_second(1, 0)
-    b_second(0, 1)
-    step(1, 2)
-    step(0, 3)
-    b_second(0, 2)
-    b_far(1)
-    b_second(1, 1)
-    step(2, 2)
-    step(1, 3)
-    b_second(0, 3)
-    b_second(1, 2)
-    step(2, 3)
-    b_last(0, 0)
-    b_last(1, 0)
-    b_second(1, 3)
-    b_last(0, 1)
-    b_last(0, 2)
-    b_last(1, 1)
+    pass_on(1, 1, 0, 7)
     b_last(1, 2)
-    b_last(0, 3)
+    pass_on(1, 1, 6, 3)
+    pass_on(1, 1, 2, 8)
     b_last(1, 3)
-    step(0, 4)
-    step(0, 5)
-    b_sibling(0)
+    pass_on(2, 1, 5, 2)
+    pass_on(2, 1, 1, 6)
     b_sibling(1)
-    compute(0, 0, 8)
-    finish(0)
-    step(1, 4)
-    step(1, 5)
-    compute(1, 0, 8)
-    finish(1)
-    step(2, 4)
-    compute(2, 0, 7)
-    step(2, 5)
-    compute(2, 7, 8)
-    finish(2)
+    compute(0, 1, 0, 4)
+    pass_on(2, 1, 0, 7)
+    compute(0, 1, 4, 7)
+    compute(0, 1, 7, 8)
+    finish(0, 1)
+    wait(1, 0, 4)
+    wait(1, 1, 4)
+    wait(1, 0, 7)
+    wait(1, 1, 7)
+    compute(1, 1, 0, 4)
+    pass_on(1, 1, 3, 9)
+    compute(1, 0, 0, 4)
+    pass_on(2, 1, 2, 8)
+    wait(1, 0, 8)
+    wait(1, 1, 8)
+    compute(1, 1, 4, 7)
+    compute(1, 0, 4, 7)
+    pass_on(2, 1, 6, 3)
+    wait(2, 0, 4)
+    wait(2, 1, 4)
+    wait(2, 0, 7)
+    wait(2, 1, 7)
+    compute(2, 1, 0, 4)
+    compute(2, 0, 0, 4)
+    wait(1, 0, 9)
+    wait(1, 1, 9)
+    compute(1, 1, 7, 8)
+    finish(1, 1)
+    pass_on(2, 1, 3, 9)
+    compute(1, 0, 7, 8)
+    finish(1, 0)
+    wait(2, 0, 8)
+    wait(2, 1, 8)
+    compute(2, 1, 4, 7)
+    compute(2, 0, 4, 7)
+    wait(2, 0, 9)
+    wait(2, 1, 9)
+    compute(2, 1, 7, 8)
+    finish(2, 1)
+    compute(2, 0, 7, 8)
+    finish(2, 0)
 
     for copy in sent:
         copy.wait_send()
-    for i in range(N):
-        store_own(i).wait()
+    for p in range(len(PARTS)):
         for n, where in AWAY:
             half = xl if n == 2 else 1 - xl
             quarter = kind if n == 1 else 1 - kind
-            arrived(out_rows(i, half, quarter), c_send.at[n, i], c_recv.at[n, i], where)
+            arrived(out_rows(p, half, quarter), c_send.at[n, p], c_recv.at[n, p], where)
 
 
 def local(waves, rotation):
@@ -346,9 +400,9 @@
     bf16 = jnp.bfloat16
     return pl.pallas_call(
         kernel,
-        out_shape=jax.ShapeDtypeStruct(waves.shape, waves.dtype),
+        out_shape=pltpu.VMEM(waves.shape, waves.dtype),
         in_specs=[pl.BlockSpec(memory_space=pl.ANY)] * 2,
-        out_specs=pl.BlockSpec(memory_space=pl.ANY),
+        out_specs=pl.BlockSpec(memory_space=pltpu.VMEM),
         scratch_shapes=[
             pltpu.VMEM((16, 2, QUARTER, W), bf16),
             pltpu.VMEM((2, 2, QUARTER, W), bf16),
@@ -356,7 +410,7 @@
             pltpu.VMEM((2, 2, QUARTER, W), bf16),
             pltpu.VMEM((2, 16, 2, 2, W, W), bf16),
             pltpu.VMEM((4, 2, QUARTER, W), bf16),
-            pltpu.VMEM((4, 2 * max(CHUNKS), 2 * W), jnp.float32),
+            pltpu.VMEM((4, 2 * QUARTER, 2 * W), jnp.float32),
             dma((4, N + 1)),
             dma((2, N)), dma((2, N)),
             dma((N, 20)), dma((N, 20)),
@@ -364,7 +418,7 @@
             dma((2, 4)), dma((2, 4)),
             dma((2, 16)), dma((2, 16)),
             dma((2, 16)), dma((2, 16)),
-            dma((4, N)), dma((4, N)), dma((N,)),
+            dma((4, N)), dma((4, N)),
         ],
         compiler_params=pltpu.CompilerParams(
             collective_id=0, has_side_effects=True, vmem_limit_bytes=60 * 1024 * 1024),

time: 98.4 us -> 86.7 us (0.88)
  the two profiles are of different devices: /device:TPU:1 before, /device:TPU:4 now
where the time goes in v3:
time: 86.7 us; the launch traced here: 86.6 us
  Pallas kernels  85.6 us (99%)
  local copies, waits for them, and re-layouts  0.97 us (1%)
    pallas_call x1, Pallas kernels, local(): pl.pallas_call(kernel, out_shape=pltpu.VMEM(waves.shape, waves.dtype), in...  85.6 us

profile of v3, /device:TPU:4, one launch (start us, length us, event | category | flops | bytes accessed | tf_op | source)
XLA Modules:
  0.0 86.6 jit_solution(14526133793467801359)
XLA Ops:
  0.0 85.6 %rotate.1 = bf16[2,1024,256]{2,1,0:T(8,128)(2,1)S(1)} custom-call(bf16[2,1024,256]{2,1,0:T(8,128)(2,1)} %waves.1, bf16[2,256,256]{2,1,0:T(8,128)(2,1)} %rot.1), custom_call_target="tpu_custom_call" | custom-call | tf_op jit(solution)/shard_map/rotate/pallas_call | solution.py:401
  85.6 1.0 %copy.4 = bf16[2,1024,256]{2,1,0:T(8,128)(2,1)} copy(bf16[2,1024,256]{2,1,0:T(8,128)(2,1)S(1)} %rotate.1) | data formatting | bytes 2097152

commit v4 on v3

--- a/solution.py
+++ b/solution.py
@@ -23,9 +23,7 @@
 def kernel(
     waves, rot, out,
     a, u, via, xs, b, cs, acc,
-    load_sem, ax_send, ax_recv, az_send, az_recv,
-    bz_send, bz_recv, b1_send, b1_recv, b2_send, b2_recv, bs_send, bs_recv,
-    c_send, c_recv,
+    load_sem, send_sem, ax_sem, az_sem, bz_sem, b1_sem, b2_sem, bs_sem, c_sem,
 ):
     xh, y, core = lax.axis_index("xh"), lax.axis_index("y"), lax.axis_index("core")
     xl, z = lax.axis_index("xl"), lax.axis_index("z")
@@ -58,15 +56,11 @@
             device_id=where, device_id_type=MESH,
         )
 
-    sent = []
-
-    def go(src, dst, send, recv, where):
-        copy = remote(src, dst, send, recv, where)
-        copy.start()
-        sent.append(copy)
-
-    def arrived(dst, send, recv, where):
-        remote(dst, dst, send, recv, where).wait_recv()
+    def go(src, dst, recv, where, group=0):
+        remote(src, dst, send_sem.at[group], recv, where).start()
+
+    def arrived(ref, recv):
+        remote(ref, ref, send_sem.at[0], recv, sibling).wait_recv()
 
     def mine(i, kb, d):
         side = xl if kb == 0 else 1 - xl
@@ -86,13 +80,18 @@
         quarter = kind if j % 2 == 0 else 1 - kind
         dst = (mine(i, 0, 0), theirs(i, 0), spare(i, 0), spare(i, 1))[j]
         return pltpu.make_async_copy(
-            waves.at[:, rows(i, half * HALF + quarter * QUARTER), :], dst, load_sem.at[j, i])
+            waves.at[:, rows(i, half * HALF + quarter * QUARTER), :], dst, load_sem.at[j // 2, i])
+
+    def both(ref, i):
+        return ref.at[:, :, rows(i), :]
+
+    def loaded(i, j):
+        pltpu.make_async_copy(both(u, i), both(u, i), load_sem.at[j, i]).wait()
 
     def swap(i):
-        load(i, 2).wait()
-        go(spare(i, 0), mine(i, 0, 0), ax_send.at[0, i], ax_recv.at[0, i], partner)
-        load(i, 3).wait()
-        go(spare(i, 1), theirs(i, 1), ax_send.at[1, i], ax_recv.at[1, i], partner)
+        loaded(i, 1)
+        go(spare(i, 0), mine(i, 0, 0), ax_sem.at[i], partner)
+        go(spare(i, 1), theirs(i, 1), ax_sem.at[i], partner)
 
     def landing(i, kb, n):
         if n == 1:
@@ -103,13 +102,18 @@
             return passing(i, kb, 2)
         return mine(i, kb, {0: -1, 2: -2, 3: -3, 4: 1, 7: 2, 8: 3, 9: 4}[n])
 
+    def mark(i, kb, n):
+        last = {4: 12, 7: 12, 8: 13, 9: 14}
+        return az_sem.at[i, last[n] if n in last else kb * 6 + (0, 1, 2, 3, 5, 6).index(n)]
+
     def over(i, kb, n, src, dst):
-        k = kb * 10 + n
-        go(src, dst, az_send.at[i, k], az_recv.at[i, k], outer if n < 4 else inner)
+        go(src, dst, mark(i, kb, n), outer if n < 4 else inner)
 
     def wait(i, kb, n):
-        k = kb * 10 + n
-        arrived(landing(i, kb, n), az_send.at[i, k], az_recv.at[i, k], outer if n < 4 else inner)
+        arrived(landing(i, kb, n), mark(i, kb, n))
+
+    def settle(i, n):
+        arrived(via.at[0:2, :, :, rows(i), :] if n == 4 else both(u, i), mark(i, 0, n))
 
     def pass_on(i, kb, got, n):
         wait(i, kb, got)
@@ -119,11 +123,9 @@
 
     def own(i, kb):
         if kb == 0:
-            load(i, 0).wait()
-            load(i, 1).wait()
+            loaded(i, 0)
         else:
-            arrived(mine(i, 1, 0), ax_send.at[0, i], ax_recv.at[0, i], partner)
-            arrived(theirs(i, 1), ax_send.at[1, i], ax_recv.at[1, i], partner)
+            arrived(both(u, i), ax_sem.at[i])
         over(i, kb, 5, theirs(i, kb), passing(i, kb, 1))
         over(i, kb, 1, mine(i, kb, 0), passing(i, kb, 0))
         over(i, kb, 4, mine(i, kb, 0), mine(i, kb, 0))
@@ -139,66 +141,54 @@
         dx, dy = (d1, d2) if g == 0 else (d2, d1)
         there = (x + dx + 4) % 4
         who = core if who is None else who
-        return b.at[g, (there // 2) * 8 + ((y + dy + 4) % 4) * 2 + who, there % 2]
+        return b.at[(g * 16 + (there // 2) * 8 + ((y + dy + 4) % 4) * 2 + who) * 2 + there % 2]
 
     load_rot = pltpu.make_async_copy(rot, block(0, 0, 0), load_sem.at[0, N])
 
     def to_sibling(g, j, k):
         ref = block(g, NEAR[j], NEAR[k])
-        go(ref, ref, bs_send.at[g, j * 4 + k], bs_recv.at[g, j * 4 + k], sibling)
+        go(ref, ref, bs_sem.at[g], sibling, 1)
 
     def to_second(g, j):
         ref = block(g, NEAR[j], 0)
         for d in range(2):
-            n = j * 4 + d
-            go(ref, ref, b2_send.at[g, n], b2_recv.at[g, n], second(g, 1 - 2 * d))
+            go(ref, ref, b2_sem.at[g, j, d], second(g, 1 - 2 * d), 1)
         to_sibling(g, j, 0)
 
     def b_out():
         load_rot.wait()
-        go(block(0, 0, 0), block(1, 0, 0), bz_send, bz_recv, outer)
+        go(block(0, 0, 0), block(1, 0, 0), bz_sem, outer)
 
     def b_start(g):
         ref = block(g, 0, 0)
         if g == 1:
-            arrived(ref, bz_send, bz_recv, outer)
+            arrived(ref, bz_sem)
         for d in range(2):
-            go(ref, ref, b1_send.at[g, d], b1_recv.at[g, d], first(g, 1 - 2 * d))
+            go(ref, ref, b1_sem.at[g, d], first(g, 1 - 2 * d))
         to_second(g, 0)
 
     def b_first(g, d):
         ref = block(g, 2 * d - 1, 0)
-        arrived(ref, b1_send.at[g, d], b1_recv.at[g, d], first(g, 1 - 2 * d))
-        part = ref.at[d]
-        go(part, part, b1_send.at[g, 2 + d], b1_recv.at[g, 2 + d], first(g, 1 - 2 * d))
+        arrived(ref, b1_sem.at[g, d])
+        go(ref.at[d], ref.at[d], b1_sem.at[g, 2], first(g, 1 - 2 * d))
         to_second(g, 1 + d)
 
     def b_far(g):
-        for d in range(2):
-            arrived(block(g, 2, 0).at[d], b1_send.at[g, 2 + d], b1_recv.at[g, 2 + d],
-                    first(g, 1 - 2 * d))
+        arrived(block(g, 2, 0), b1_sem.at[g, 2])
         to_second(g, 3)
 
     def b_second(g, j, d):
-        n = j * 4 + d
         ref = block(g, NEAR[j], 2 * d - 1)
-        arrived(ref, b2_send.at[g, n], b2_recv.at[g, n], second(g, 1 - 2 * d))
-        part = ref.at[d]
-        go(part, part, b2_send.at[g, n + 2], b2_recv.at[g, n + 2], second(g, 1 - 2 * d))
+        arrived(ref, b2_sem.at[g, j, d])
+        go(ref.at[d], ref.at[d], b2_sem.at[g, j, 2], second(g, 1 - 2 * d), 1)
         to_sibling(g, j, 1 + d)
 
     def b_last(g, j):
-        for d in range(2):
-            n = j * 4 + 2 + d
-            arrived(block(g, NEAR[j], 2).at[d], b2_send.at[g, n], b2_recv.at[g, n],
-                    second(g, 1 - 2 * d))
+        arrived(block(g, NEAR[j], 2), b2_sem.at[g, j, 2])
         to_sibling(g, j, 3)
 
     def b_sibling(g):
-        for j in range(4):
-            for k in range(4):
-                arrived(block(g, NEAR[j], NEAR[k], 1 - core),
-                        bs_send.at[g, j * 4 + k], bs_recv.at[g, j * 4 + k], sibling)
+        arrived(b.at[0:16], bs_sem.at[g])
 
     def compute(p, g, low, high):
         base, r = PARTS[p]
@@ -215,7 +205,7 @@
                     total = acc[g * 2 + n, pl.ds(2 * base, 2 * r), cd * W : (cd + 1) * W]
                     for side in (0, 1):
                         total = total + jnp.dot(
-                            lhs[side], b[g, side * 8 + place, which, cd],
+                            lhs[side], b[(g * 16 + side * 8 + place) * 2 + which, cd],
                             preferred_element_type=jnp.float32)
                     acc[g * 2 + n, pl.ds(2 * base, 2 * r), cd * W : (cd + 1) * W] = total
             return carry
@@ -242,7 +232,7 @@
             dst[1] = (acc[n, top, W:] + acc[n, low, :W]).astype(jnp.bfloat16)
         for n, where in AWAY:
             if n // 2 == g:
-                go(result(n, p), out_rows(p, xl, kind), c_send.at[n, p], c_recv.at[n, p], where)
+                go(result(n, p), out_rows(p, xl, kind), c_sem, where)
 
     for i in range(N):
         load(i, 0).start()
@@ -320,17 +310,12 @@
     b_second(1, 3, 0)
     b_second(1, 3, 1)
     b_sibling(0)
-    wait(0, 0, 4)
-    wait(0, 1, 4)
-    wait(0, 0, 7)
-    wait(0, 1, 7)
+    settle(0, 4)
     compute(0, 0, 0, 4)
     pass_on(1, 1, 1, 6)
-    wait(0, 0, 8)
-    wait(0, 1, 8)
+    settle(0, 8)
     compute(0, 0, 4, 7)
-    wait(0, 0, 9)
-    wait(0, 1, 9)
+    settle(0, 9)
     compute(0, 0, 7, 8)
     finish(0, 0)
     b_last(1, 1)
@@ -349,50 +334,36 @@
     compute(0, 1, 4, 7)
     compute(0, 1, 7, 8)
     finish(0, 1)
-    wait(1, 0, 4)
-    wait(1, 1, 4)
-    wait(1, 0, 7)
-    wait(1, 1, 7)
+    settle(1, 4)
     compute(1, 1, 0, 4)
     pass_on(1, 1, 3, 9)
     compute(1, 0, 0, 4)
     pass_on(2, 1, 2, 8)
-    wait(1, 0, 8)
-    wait(1, 1, 8)
+    settle(1, 8)
     compute(1, 1, 4, 7)
     compute(1, 0, 4, 7)
     pass_on(2, 1, 6, 3)
-    wait(2, 0, 4)
-    wait(2, 1, 4)
-    wait(2, 0, 7)
-    wait(2, 1, 7)
+    settle(2, 4)
     compute(2, 1, 0, 4)
     compute(2, 0, 0, 4)
-    wait(1, 0, 9)
-    wait(1, 1, 9)
+    settle(1, 9)
     compute(1, 1, 7, 8)
     finish(1, 1)
     pass_on(2, 1, 3, 9)
     compute(1, 0, 7, 8)
     finish(1, 0)
-    wait(2, 0, 8)
-    wait(2, 1, 8)
+    settle(2, 8)
     compute(2, 1, 4, 7)
     compute(2, 0, 4, 7)
-    wait(2, 0, 9)
-    wait(2, 1, 9)
+    settle(2, 9)
     compute(2, 1, 7, 8)
     finish(2, 1)
     compute(2, 0, 7, 8)
     finish(2, 0)
 
-    for copy in sent:
-        copy.wait_send()
-    for p in range(len(PARTS)):
-        for n, where in AWAY:
-            half = xl if n == 2 else 1 - xl
-            quarter = kind if n == 1 else 1 - kind
-            arrived(out_rows(p, half, quarter), c_send.at[n, p], c_recv.at[n, p], where)
+    remote(b.at[0:32], b.at[0:32], send_sem.at[0], c_sem, sibling).wait_send()
+    remote(b.at[0:56], b.at[0:56], send_sem.at[1], c_sem, sibling).wait_send()
+    arrived(cs.at[0:3], c_sem)
 
 
 def local(waves, rotation):
@@ -408,17 +379,11 @@
             pltpu.VMEM((2, 2, QUARTER, W), bf16),
             pltpu.VMEM((3, 2, 2, QUARTER, W), bf16),
             pltpu.VMEM((2, 2, QUARTER, W), bf16),
-            pltpu.VMEM((2, 16, 2, 2, W, W), bf16),
+            pltpu.VMEM((64, 2, W, W), bf16),
             pltpu.VMEM((4, 2, QUARTER, W), bf16),
             pltpu.VMEM((4, 2 * QUARTER, 2 * W), jnp.float32),
-            dma((4, N + 1)),
-            dma((2, N)), dma((2, N)),
-            dma((N, 20)), dma((N, 20)),
-            dma, dma,
-            dma((2, 4)), dma((2, 4)),
-            dma((2, 16)), dma((2, 16)),
-            dma((2, 16)), dma((2, 16)),
-            dma((4, N)), dma((4, N)),
+            dma((2, N + 1)), dma((2,)), dma((N,)), dma((N, 15)), dma,
+            dma((2, 3)), dma((2, 4, 3)), dma((2,)), dma,
         ],
         compiler_params=pltpu.CompilerParams(
             collective_id=0, has_side_effects=True, vmem_limit_bytes=60 * 1024 * 1024),

time: 86.7 us -> 84.7 us (0.977)
  Pallas kernels: 85.6 us -> 83.6 us
    pallas_call x1, Pallas kernels: 85.6 us -> 83.6 us  [local(): pl.pallas_call(kernel, out_shape=pltpu.VMEM(waves.shape, waves.dtype), in...]
where the time goes in v4:
time: 84.7 us; the launch traced here: 84.6 us
  Pallas kernels  83.6 us (99%)
  local copies, waits for them, and re-layouts  0.97 us (1%)
    pallas_call x1, Pallas kernels, local(): pl.pallas_call(kernel, out_shape=pltpu.VMEM(waves.shape, waves.dtype), in...  83.6 us

profile of v4, /device:TPU:4, one launch (start us, length us, event | category | flops | bytes accessed | tf_op | source)
XLA Modules:
  0.0 84.6 jit_solution(5552644291515781167)
XLA Ops:
  0.0 83.6 %rotate.1 = bf16[2,1024,256]{2,1,0:T(8,128)(2,1)S(1)} custom-call(bf16[2,1024,256]{2,1,0:T(8,128)(2,1)} %waves.1, bf16[2,256,256]{2,1,0:T(8,128)(2,1)} %rot.1), custom_call_target="tpu_custom_call" | custom-call | tf_op jit(solution)/shard_map/rotate/pallas_call | solution.py:372
  83.6 1.0 %copy.4 = bf16[2,1024,256]{2,1,0:T(8,128)(2,1)} copy(bf16[2,1024,256]{2,1,0:T(8,128)(2,1)S(1)} %rotate.1) | data formatting | bytes 2097152

commit v5 on v4

--- a/solution.py
+++ b/solution.py
@@ -234,6 +234,9 @@
             if n // 2 == g:
                 go(result(n, p), out_rows(p, xl, kind), c_sem, where)
 
+    barrier = pltpu.get_barrier_semaphore()
+    for where in (at_x(1), at_x(-1), at_y(1), at_y(-1), inner, outer, across, sibling):
+        pl.semaphore_signal(barrier, inc=1, device_id=where, device_id_type=MESH)
     for i in range(N):
         load(i, 0).start()
         load(i, 1).start()
@@ -241,10 +244,6 @@
         load(i, 3).start()
         if i == 0:
             load_rot.start()
-
-    barrier = pltpu.get_barrier_semaphore()
-    for where in (at_x(1), at_x(-1), at_y(1), at_y(-1), inner, outer, across, sibling):
-        pl.semaphore_signal(barrier, inc=1, device_id=where, device_id_type=MESH)
     pl.semaphore_wait(barrier, 8)
 
     b_out()

time: 84.7 us -> 84.6 us (level)
  no operation moved by 1% of the time
where the time goes in v5:
time: 84.6 us
  Pallas kernels  83.6 us (99%)
  local copies, waits for them, and re-layouts  0.97 us (1%)
    pallas_call x1, Pallas kernels, local(): pl.pallas_call(kernel, out_shape=pltpu.VMEM(waves.shape, waves.dtype), in...  83.6 us

profile of v5, /device:TPU:4, one launch (start us, length us, event | category | flops | bytes accessed | tf_op | source)
XLA Modules:
  0.0 84.6 jit_solution(13216891743060459220)
XLA Ops:
  0.0 83.6 %rotate.1 = bf16[2,1024,256]{2,1,0:T(8,128)(2,1)S(1)} custom-call(bf16[2,1024,256]{2,1,0:T(8,128)(2,1)} %waves.1, bf16[2,256,256]{2,1,0:T(8,128)(2,1)} %rot.1), custom_call_target="tpu_custom_call" | custom-call | tf_op jit(solution)/shard_map/rotate/pallas_call | solution.py:371
  83.6 1.0 %copy.4 = bf16[2,1024,256]{2,1,0:T(8,128)(2,1)} copy(bf16[2,1024,256]{2,1,0:T(8,128)(2,1)S(1)} %rotate.1) | data formatting | bytes 2097152
